TPU v7x, 16 devices: a whole 2x2x2 slice. The times are simulated.
16 devices in a mesh: rep: 1, dp: 16 (over x, y, z, core).
Axes of the slice: x: 2, y: 2, z: 2, core: 2. Of those that a mesh axis runs over, the one named last changes fastest.
Arguments:
- a: bfloat16 [16, 4, 4096, 1024], P(('rep', 'dp'))
- g: bfloat16 [16, 4, 4096, 3328], P(('rep', 'dp'))
Outputs:
- output: bfloat16 [4, 1024, 3328], P('rep')
All inputs are finite; a program needn't handle non-finite values.
Results may differ from a plain program's by a relative error of at most 0.012.
Values are sent between devices in bfloat16 or wider.
A program may use at most 2 GiB of HBM per device.

v0:
```python
import jax
import jax.numpy as jnp


def solution(mesh):
    groups = mesh.shape["rep"]

    def step(a, g):
        a, g = (t.reshape(groups, -1, *t.shape[1:]) for t in (a, g))
        sums = jnp.einsum("rsntd,rsntf->rndf", a, g, preferred_element_type=jnp.float32)
        return sums.astype(jnp.bfloat16).reshape(-1, *sums.shape[2:])

    return step
```

profile of v0, /device:TPU:0, one launch (start us, length us, event | category | flops | bytes accessed | tf_op | source)
XLA Modules:
  0.0 625.2 jit_solution(6830592942670186284)
XLA Ops:
  0.0 129.7 %fusion = f32[4,1024,3328]{2,1,0:T(8,128)} fusion(bf16[1,4,4096,3328]{3,2,1,0:T(8,128)(2,1)} %param.1, bf16[1,4,4096,1024]{3,2,1,0:T(8,128)(2,1)} %param), kind=kOutput, calls=%fused_computation | convolution fusion | flops 111669149696 | bytes 197132288 | tf_op jit(solution)/rsntd,rsntf->rndf/dot_general | solution.py:10
  129.7 495.5 %all-reduce.2 = bf16[4,1024,3328]{2,1,0:T(8,128)(2,1)} all-reduce(f32[4,1024,3328]{2,1,0:T(8,128)} %fusion), channel_id=1, replica_groups=mesh['axis_0'=16] {'axis_0'}, use_global_device_ids=true, to_apply=%add.clone | all-reduce | flops 13631488 | bytes 81788928 | tf_op jit(solution)/rsntd,rsntf->rndf/dot_general | solution.py:10
where the time goes:
time: 625 us
  blocking collectives  495 us (79%)
  matrix products  130 us (21%)
    dot_general x1, blocking collectives, step(): jnp.einsum('rsntd,rsntf->rndf', a, g, preferred_element_type=jnp.float32)  495 us
    dot_general x1, matrix products, step(): jnp.einsum('rsntd,rsntf->rndf', a, g, preferred_element_type=jnp.float32)  130 us

commit v1 on v0

v1 whole, which is shorter than its diff:
```python
import functools

import jax
import jax.numpy as jnp
from jax import lax
from jax.experimental import pallas as pl
from jax.experimental.pallas import tpu as pltpu
from jax.sharding import PartitionSpec as P

MESH = pl.DeviceIdType.MESH
W = 256
KC = 256
STAGE = 8
RS0, RS1, RS2, AG0, AG1, AG2, AG3, END = 2, 5, 7, 9, 11, 16, 19, 21
S_GO, S_GOT, S_RS, S_AG = 3, 4, 6, 12


def kernel(
    a, g, out, aT, stage, gbuf, full, own, core_s, core_r, k1, s1, r1, k2, s2, r2, k3, s3, r3,
    a_sem, g_sem, o_sem, send_c, recv_c, send_rs, recv_rs, send_ag, recv_ag,
):
    _, n_mat, depth, rows = a.shape
    tiles = g.shape[-1] // W
    units, chunks = n_mat * tiles, depth // KC
    half = rows // 2
    f32, bf16 = jnp.float32, jnp.bfloat16

    me = lax.axis_index("dp")
    core, z, y, x = me % 2, (me // 2) % 2, (me // 4) % 2, me // 8
    other = me + 1 - 2 * core
    near = (me + 8 - 16 * x, me + 4 - 8 * y, me + 2 - 4 * z)

    barrier = pltpu.get_barrier_semaphore()
    for d in (other, *near):
        pl.semaphore_signal(barrier, inc=1, device_id={"dp": d}, device_id_type=MESH)

    def pick(k, options):
        return jnp.where(k == 0, options[0], jnp.where(k == 1, options[1], options[2]))

    def axis(u, turn):
        k = (u + 2 * turn) % 3
        return pick(k, near), pick(k, (x, y, z))

    def spot(u, level):
        base, size = core * half, half
        for turn in range(level):
            size //= 2
            base = base + axis(u, turn)[1] * size
        base = pl.multiple_of(base, size)
        column = pl.multiple_of((u % tiles) * W, W)
        return full.at[u // tiles, pl.ds(base, size), pl.ds(column, W)]

    def remote(src, dst, send, recv, to):
        return pltpu.make_async_remote_copy(
            src_ref=src, dst_ref=dst, send_sem=send, recv_sem=recv, device_id={"dp": to}, device_id_type=MESH
        )

    def swap(u):
        return remote(core_s.at[u % S_GO], core_r.at[u % S_GOT], send_c.at[u % S_GO], recv_c.at[u % S_GOT], other)

    def scatter(u, turn):
        i = u % S_RS
        src, dst = ((s1, r1), (s2, r2), (s3, r3))[turn]
        return remote(src.at[i], dst.at[i], send_rs.at[turn, i], recv_rs.at[turn, i], axis(u, turn)[0])

    def gather(u, turn):
        i = u % S_AG
        place = spot(u, 3 - turn)
        to = other if turn == 3 else axis(u, 2 - turn)[0]
        return remote(place, place, send_ag.at[turn, i], recv_ag.at[turn, i], to)

    def store_out(u):
        column = pl.multiple_of((u % tiles) * W, W)
        at = (u // tiles, slice(None), pl.ds(column, W))
        return pltpu.make_async_copy(full.at[at], out.at[at], o_sem.at[u % 2])

    def load_g(u):
        column = pl.multiple_of((u % tiles) * W, W)
        return pltpu.make_async_copy(g.at[0, u // tiles, :, pl.ds(column, W)], gbuf.at[u % 3], g_sem.at[u % 3])

    def load_a(n, q):
        row = pl.multiple_of(q * KC, KC)
        return pltpu.make_async_copy(a.at[0, n, pl.ds(row, KC), :], stage.at[q % STAGE], a_sem.at[q % STAGE])

    def turn_a(n, q):
        load_a(n, q).wait()
        aT[n % 2, :, pl.ds(pl.multiple_of(q * KC, KC), KC)] = stage[q % STAGE].T

    def halve(u, turn, mine, came, keep, send):
        size = came.shape[0] // 2
        bit = axis(u, turn)[1]
        theirs = pl.ds(pl.multiple_of((1 - bit) * size, size), size)
        ours = pl.ds(pl.multiple_of(bit * size, size), size)
        send[...] = (mine[theirs, :] + came[theirs, :].astype(f32)).astype(bf16)
        scatter(u, turn).start()
        keep[...] = mine[ours, :] + came[ours, :].astype(f32)

    def rs0(u):
        swap(u).wait_recv()
        halve(u, 0, own, core_r.at[u % S_GOT], k1.at[u % 3], s1.at[u % S_RS])

    def rs1(u):
        scatter(u, 0).wait_recv()
        halve(u, 1, k1.at[u % 3], r1.at[u % S_RS], k2.at[u % 3], s2.at[u % S_RS])
        swap(u).wait_send()

    def rs2(u):
        scatter(u, 1).wait_recv()
        halve(u, 2, k2.at[u % 3], r2.at[u % S_RS], k3.at[u % 3], s3.at[u % S_RS])

    def ag0(u):
        scatter(u, 2).wait_recv()
        spot(u, 3)[...] = (k3[u % 3] + r3[u % S_RS].astype(f32)).astype(bf16)
        gather(u, 0).start()
        scatter(u, 0).wait_send()

    def ag1(u):
        gather(u, 0).wait_recv()
        gather(u, 1).start()
        scatter(u, 1).wait_send()

    def ag2(u):
        gather(u, 1).wait_recv()
        gather(u, 2).start()
        scatter(u, 2).wait_send()
        gather(u, 0).wait_send()

    def ag3(u):
        gather(u, 2).wait_recv()
        gather(u, 3).start()
        gather(u, 1).wait_send()

    def end(u):
        gather(u, 3).wait_recv()
        store_out(u).start()
        gather(u, 2).wait_send()
        gather(u, 3).wait_send()

    def end2(u):
        store_out(u).wait()

    phases = (
        (END + 2, end2), (END, end), (AG3, ag3), (AG2, ag2), (AG1, ag1), (AG0, ag0), (RS2, rs2), (RS1, rs1), (RS0, rs0)
    )

    ahead = min(STAGE, chunks)
    for q in range(ahead):
        load_a(0, q).start()
    load_g(0).start()
    load_g(1).start()

    def first(q, _):
        turn_a(0, q)

        @pl.when(q + ahead < chunks)
        def _():
            load_a(0, q + ahead).start()

    lax.fori_loop(0, chunks, first, None)
    pl.semaphore_wait(barrier, 4)

    def matmul(u, base):
        lhs = aT[(u // tiles) % 2, pl.ds(pl.multiple_of(base, half), half), :]
        return jnp.dot(lhs, gbuf[u % 3], preferred_element_type=f32)

    def step(t, _):
        for parity in range(2):
            for delay, phase in phases:
                if delay % 2 == parity:
                    u = t - delay // 2

                    @pl.when(jnp.logical_and(u >= 0, u < units))
                    def _(u=u, phase=phase):
                        phase(u)

            n, q = t // tiles + 1, 2 * (t % tiles) + parity

            @pl.when(jnp.logical_and(n < n_mat, q < chunks))
            def _():
                load_a(n, q).start()

            @pl.when(jnp.logical_and(n < n_mat, jnp.logical_and(q >= 2, q < chunks + 2)))
            def _():
                turn_a(n, q - 2)

            @pl.when(t < units)
            def _():
                if parity == 0:
                    load_g(t).wait()

                    @pl.when(t + 2 < units)
                    def _():
                        load_g(t + 2).start()

                    core_s[t % S_GO] = matmul(t, (1 - core) * half).astype(bf16)
                    swap(t).start()
                else:
                    own[...] = matmul(t, core * half)

    lax.fori_loop(0, units + END // 2 + 2, step, None)


def solution(mesh):
    def step(a, g):
        _, n_mat, depth, rows = a.shape
        columns = g.shape[-1]
        half = rows // 2
        f32, bf16 = jnp.float32, jnp.bfloat16
        q1, q2, q3 = half // 2, half // 4, half // 8
        DMA = pltpu.SemaphoreType.DMA
        return pl.pallas_call(
            kernel,
            name="grad_sums",
            out_shape=jax.ShapeDtypeStruct((n_mat, rows, columns), bf16),
            in_specs=[pl.BlockSpec(memory_space=pl.ANY)] * 2,
            out_specs=pl.BlockSpec(memory_space=pl.ANY),
            scratch_shapes=[
                pltpu.VMEM((2, rows, depth), bf16),
                pltpu.VMEM((STAGE, KC, rows), bf16),
                pltpu.VMEM((3, depth, W), bf16),
                pltpu.VMEM((n_mat, rows, columns), bf16),
                pltpu.VMEM((half, W), f32),
                pltpu.VMEM((S_GO, half, W), bf16),
                pltpu.VMEM((S_GOT, half, W), bf16),
                pltpu.VMEM((3, q1, W), f32),
                pltpu.VMEM((S_RS, q1, W), bf16),
                pltpu.VMEM((S_RS, q1, W), bf16),
                pltpu.VMEM((3, q2, W), f32),
                pltpu.VMEM((S_RS, q2, W), bf16),
                pltpu.VMEM((S_RS, q2, W), bf16),
                pltpu.VMEM((3, q3, W), f32),
                pltpu.VMEM((S_RS, q3, W), bf16),
                pltpu.VMEM((S_RS, q3, W), bf16),
                DMA((STAGE,)),
                DMA((3,)),
                DMA((2,)),
                DMA((S_GO,)),
                DMA((S_GOT,)),
                DMA((3, S_RS)),
                DMA((3, S_RS)),
                DMA((4, S_AG)),
                DMA((4, S_AG)),
            ],
            compiler_params=pltpu.CompilerParams(
                collective_id=0, has_side_effects=True, vmem_limit_bytes=67043328
            ),
            cost_estimate=pl.CostEstimate(
                flops=2 * n_mat * depth * rows * columns, bytes_accessed=2 * n_mat * (depth * (rows + columns)), transcendentals=0
            ),
        )(a, g)

    return jax.shard_map(
        step,
        mesh=mesh,
        in_specs=(P(("rep", "dp")), P(("rep", "dp"))),
        out_specs=P("rep"),
        check_vma=False,
    )
```

time: 625 us -> 282 us (0.45)
  blocking collectives: 495 us -> 0 us
  Pallas kernels: 0 us -> 262 us
  matrix products: 130 us -> 0 us
  local copies, waits for them, and re-layouts: 0 us -> 19.3 us
    dot_general x1 -> x0, blocking collectives: 495 us -> none  [step(): jnp.einsum('rsntd,rsntf->rndf', a, g, preferred_element_type=jnp.float32)]
    pallas_call x0 -> x1, Pallas kernels: none -> 262 us  [step(): pl.pallas_call(kernel, name='grad_sums', out_shape=jax.ShapeDtypeStruct((...]
    dot_general x1 -> x0, matrix products: 130 us -> none  [step(): jnp.einsum('rsntd,rsntf->rndf', a, g, preferred_element_type=jnp.float32)]
    unnamed x0 -> x1, local copies, waits for them, and re-layouts: none -> 19.3 us
where the time goes in v1:
time: 282 us; the launch traced here: 281 us
  Pallas kernels  262 us (93%)
  local copies, waits for them, and re-layouts  19.3 us (7%)
    pallas_call x1, Pallas kernels, step(): pl.pallas_call(kernel, name='grad_sums', out_shape=jax.ShapeDtypeStruct((...  262 us
    unnamed x1, local copies, waits for them, and re-layouts  19.3 us

profile of v1, /device:TPU:0, one launch (start us, length us, event | category | flops | bytes accessed | tf_op | source)
XLA Modules:
  0.0 281.1 jit_solution(12536197811752673546)
XLA Ops:
  0.0 261.8 %grad_sums.1 = bf16[4,1024,3328]{2,1,0:T(8,128)(2,1)} custom-call(bf16[1,4,4096,1024]{3,2,1,0:T(8,128)(2,1)} %a.1, bf16[1,4,4096,3328]{3,2,1,0:T(8,128)(2,1)} %g.1), custom_call_target="tpu_custom_call" | custom-call | flops 111669149696 | bytes 142606336 | tf_op jit(solution)/shard_map/grad_sums/pallas_call | solution.py:211
  261.8 19.3 %copy.4 = bf16[4,1024,3328]{2,1,0:T(8,128)(2,1)} copy(bf16[4,1024,3328]{2,1,0:T(8,128)(2,1)} %grad_sums.1) | data formatting | bytes 54525952

commit v2 on v1

v2 whole, which is shorter than its diff:
```python
import functools

import jax
import jax.numpy as jnp
from jax import lax
from jax.experimental import pallas as pl
from jax.experimental.pallas import tpu as pltpu
from jax.sharding import PartitionSpec as P

MESH = pl.DeviceIdType.MESH


def rem(x, n):
    return lax.rem(jnp.int32(x), jnp.int32(n))


def div(x, n):
    return lax.div(jnp.int32(x), jnp.int32(n))


class Unit:
    def __init__(self, three, plus):
        self.third = plus % 3
        self.three = three + plus // 3
        self.at = 3 * three + plus


W = 256
KC = 256
STAGE = 4
RS0, RS1, RS2, AG0, AG1, AG2, AG3, END = 2, 6, 9, 13, 19, 24, 33, 40
SPIN = 1
S_GO, S_GOT, S_RS, S_AG, S_END, K1, K2, K3 = 3, 6, 9, 18, 21, 3, 3, 3


def kernel(
    a, g, full, aT, stage, gbuf, own, core_s, core_r, k1, s1, r1, k2, s2, r2, k3, s3, r3,
    a_sem, g_sem, send_c, recv_c, send_rs, recv_rs, send_ag, recv_ag,
    send_end, recv_end,
):
    _, n_mat, depth, rows = a.shape
    tiles = g.shape[-1] // W
    units, chunks = n_mat * tiles, depth // KC
    half = rows // 2
    f32, bf16 = jnp.float32, jnp.bfloat16

    me = lax.axis_index("dp")
    core, z, y, x = rem(me, 2), rem(div(me, 2), 2), rem(div(me, 4), 2), div(me, 8)
    other = me + 1 - 2 * core
    near = (me + 8 - 16 * x, me + 4 - 8 * y, me + 2 - 4 * z)

    barrier = pltpu.get_barrier_semaphore()
    for d in (other, *near):
        pl.semaphore_signal(barrier, inc=1, device_id={"dp": d}, device_id_type=MESH)

    def axis(u, turn):
        k = (u.third + SPIN * turn) % 3
        return near[k], (x, y, z)[k]

    def slot(u, n):
        return u.third if n == 3 else 3 * rem(u.three, n // 3) + u.third

    def bounds(u, level):
        base, size = core * half, half
        for turn in range(level):
            size //= 2
            base = base + axis(u, turn)[1] * size
        return base, size

    def rows_of(u, base, size):
        column = pl.multiple_of(rem(u.at, tiles) * W, W)
        return full.at[div(u.at, tiles), pl.ds(pl.multiple_of(base, size), size), pl.ds(column, W)]

    def remote(src, dst, send, recv, to):
        return pltpu.make_async_remote_copy(
            src_ref=src, dst_ref=dst, send_sem=send, recv_sem=recv, device_id={"dp": to}, device_id_type=MESH
        )

    def swap(u):
        return remote(core_s.at[slot(u, S_GO)], core_r.at[slot(u, S_GOT)], send_c.at[slot(u, S_GO)], recv_c.at[slot(u, S_GOT)], other)

    def scatter(u, turn):
        i = slot(u, S_RS)
        src, dst = ((s1, r1), (s2, r2), (s3, r3))[turn]
        return remote(src.at[i], dst.at[i], send_rs.at[turn, i], recv_rs.at[turn, i], axis(u, turn)[0])

    def gather(u, kind):
        if kind == 6:
            i = slot(u, S_END)
            place = rows_of(u, core * half, half)
            return remote(place, place, send_end.at[i], recv_end.at[i], other)
        i = slot(u, S_AG)
        turn = (2, 1, 0, 1, 0, 0)[kind]
        base, size = bounds(u, 3)
        if kind in (3, 4):
            base = base + (1 - 2 * axis(u, 2)[1]) * size
        if kind == 5:
            base, size = bounds(u, 2)
            base = base + (1 - 2 * axis(u, 1)[1]) * size
        place = rows_of(u, base, size)
        return remote(place, place, send_ag.at[kind, i], recv_ag.at[kind, i], axis(u, turn)[0])

    def load_g(u):
        column = pl.multiple_of((rem(u.at, tiles)) * W, W)
        return pltpu.make_async_copy(g.at[0, div(u.at, tiles), :, pl.ds(column, W)], gbuf.at[slot(u, 3)], g_sem.at[slot(u, 3)])

    def load_a(n, q):
        row = pl.multiple_of(q * KC, KC)
        return pltpu.make_async_copy(a.at[0, n, pl.ds(row, KC), :], stage.at[rem(q, STAGE)], a_sem.at[rem(q, STAGE)])

    def turn_a(n, q):
        load_a(n, q).wait()
        aT[rem(n, 2), :, pl.ds(pl.multiple_of(q * KC, KC), KC)] = stage[rem(q, STAGE)].T

    def halve(u, turn, mine, came, keep, send):
        size = came.shape[0] // 2
        bit = axis(u, turn)[1]
        theirs = pl.ds(pl.multiple_of((1 - bit) * size, size), size)
        ours = pl.ds(pl.multiple_of(bit * size, size), size)
        send[...] = (mine[theirs, :] + came[theirs, :].astype(f32)).astype(bf16)
        scatter(u, turn).start()
        keep[...] = mine[ours, :] + came[ours, :].astype(f32)

    def rs0(u):
        swap(u).wait_recv()
        swap(u).wait_send()
        halve(u, 0, own, core_r.at[slot(u, S_GOT)], k1.at[slot(u, K1)], s1.at[slot(u, S_RS)])

    def rs1(u):
        scatter(u, 0).wait_recv()
        halve(u, 1, k1.at[slot(u, K1)], r1.at[slot(u, S_RS)], k2.at[slot(u, K2)], s2.at[slot(u, S_RS)])

    def rs2(u):
        scatter(u, 1).wait_recv()
        halve(u, 2, k2.at[slot(u, K2)], r2.at[slot(u, S_RS)], k3.at[slot(u, K3)], s3.at[slot(u, S_RS)])

    def ag0(u):
        scatter(u, 2).wait_recv()
        rows_of(u, *bounds(u, 3))[...] = (k3[slot(u, K3)] + r3[slot(u, S_RS)].astype(f32)).astype(bf16)
        for kind in (0, 1, 2):
            gather(u, kind).start()
        scatter(u, 0).wait_send()

    def ag1(u):
        gather(u, 0).wait_recv()
        gather(u, 3).start()
        gather(u, 4).start()
        scatter(u, 1).wait_send()

    def ag2(u):
        gather(u, 1).wait_recv()
        gather(u, 3).wait_recv()
        gather(u, 5).start()
        scatter(u, 2).wait_send()

    def ag3(u):
        for kind in (2, 4, 5):
            gather(u, kind).wait_recv()
        gather(u, 6).start()

    def end(u):
        gather(u, 6).wait_recv()
        for kind in range(7):
            gather(u, kind).wait_send()

    phases = (
        (END, end), (AG3, ag3), (AG2, ag2), (AG1, ag1), (AG0, ag0), (RS2, rs2), (RS1, rs1), (RS0, rs0)
    )

    side = rows // KC

    def raw(q):
        return pl.ds(pl.multiple_of((rem(q, side)) * KC, KC), KC), pl.ds(pl.multiple_of((div(q, side)) * rows, rows), rows)

    def load_first(q):
        row = pl.multiple_of(q * KC, KC)
        at = raw(q)
        return pltpu.make_async_copy(a.at[0, 0, pl.ds(row, KC), :], aT.at[1, at[0], at[1]], a_sem.at[q])

    for q in range(chunks):
        load_first(q).start()
    load_g(Unit(0, 0)).start()
    load_g(Unit(0, 1)).start()

    def first(q, _):
        load_first(q).wait()
        at = raw(q)
        aT[0, :, pl.ds(pl.multiple_of(q * KC, KC), KC)] = aT[1, at[0], at[1]].T

    lax.fori_loop(0, chunks, first, None)
    pl.semaphore_wait(barrier, 4)

    def matmul(u, base):
        lhs = aT[rem(div(u.at, tiles), 2), pl.ds(pl.multiple_of(base, half), half), :]
        return jnp.dot(lhs, gbuf[slot(u, 3)], preferred_element_type=f32)

    def three(i, _):
        for plus in range(3):
            for parity in range(2):
                half_step(i, plus, parity)

    def half_step(i, plus, parity):
        unit = Unit(i, plus)
        t = unit.at
        for delay, phase in phases:
            if delay % 2 == parity:
                u = Unit(i, plus - delay // 2)

                @pl.when(jnp.logical_and(u.at >= 0, u.at < units))
                def _(u=u, phase=phase):
                    phase(u)

        n, q = div(t, tiles) + 1, 2 * rem(t, tiles) + parity - (2 * tiles - chunks - 2)

        @pl.when(jnp.logical_and(n < n_mat, jnp.logical_and(q >= 0, q < chunks)))
        def _():
            load_a(n, q).start()

        @pl.when(jnp.logical_and(n < n_mat, jnp.logical_and(q >= 2, q < chunks + 2)))
        def _():
            turn_a(n, q - 2)

        @pl.when(t < units)
        def _():
            if parity == 0:
                load_g(unit).wait()

                @pl.when(t + 2 < units)
                def _():
                    load_g(Unit(i, plus + 2)).start()

                core_s[slot(unit, S_GO)] = matmul(unit, (1 - core) * half).astype(bf16)
                swap(unit).start()
            else:
                own[...] = matmul(unit, core * half)

    lax.fori_loop(0, (units + END // 2 + 2) // 3 + 1, three, None)


def solution(mesh):
    def step(a, g):
        _, n_mat, depth, rows = a.shape
        columns = g.shape[-1]
        half = rows // 2
        f32, bf16 = jnp.float32, jnp.bfloat16
        q1, q2, q3 = half // 2, half // 4, half // 8
        DMA = pltpu.SemaphoreType.DMA
        sums = pl.pallas_call(
            kernel,
            name="grad_sums",
            out_shape=pltpu.VMEM((n_mat, rows, columns), bf16),
            in_specs=[pl.BlockSpec(memory_space=pl.ANY)] * 2,
            out_specs=pl.BlockSpec(memory_space=pltpu.VMEM),
            scratch_shapes=[
                pltpu.VMEM((2, rows, depth), bf16),
                pltpu.VMEM((STAGE, KC, rows), bf16),
                pltpu.VMEM((3, depth, W), bf16),
                pltpu.VMEM((half, W), f32),
                pltpu.VMEM((S_GO, half, W), bf16),
                pltpu.VMEM((S_GOT, half, W), bf16),
                pltpu.VMEM((K1, q1, W), f32),
                pltpu.VMEM((S_RS, q1, W), bf16),
                pltpu.VMEM((S_RS, q1, W), bf16),
                pltpu.VMEM((K2, q2, W), f32),
                pltpu.VMEM((S_RS, q2, W), bf16),
                pltpu.VMEM((S_RS, q2, W), bf16),
                pltpu.VMEM((K3, q3, W), f32),
                pltpu.VMEM((S_RS, q3, W), bf16),
                pltpu.VMEM((S_RS, q3, W), bf16),
                DMA((depth // KC,)),
                DMA((3,)),
                DMA((S_GO,)),
                DMA((S_GOT,)),
                DMA((3, S_RS)),
                DMA((3, S_RS)),
                DMA((6, S_AG)),
                DMA((6, S_AG)),
                DMA((S_END,)),
                DMA((S_END,)),
            ],
            compiler_params=pltpu.CompilerParams(
                collective_id=0, has_side_effects=True, vmem_limit_bytes=34 * 2**20
            ),
            cost_estimate=pl.CostEstimate(
                flops=2 * n_mat * depth * rows * columns, bytes_accessed=2 * n_mat * (depth * (rows + columns)), transcendentals=0
            ),
        )(a, g)

        def place(src, dst, sem):
            copy = pltpu.make_async_copy(src, dst, sem)
            copy.start()
            copy.wait()

        return pl.pallas_call(
            place,
            name="place",
            out_shape=jax.ShapeDtypeStruct(sums.shape, sums.dtype),
            in_specs=[pl.BlockSpec(memory_space=pltpu.VMEM)],
            out_specs=pl.BlockSpec(memory_space=pl.ANY),
            scratch_shapes=[DMA],
            compiler_params=pltpu.CompilerParams(vmem_limit_bytes=2**20),
        )(sums)

    return jax.shard_map(
        step,
        mesh=mesh,
        in_specs=(P(("rep", "dp")), P(("rep", "dp"))),
        out_specs=P("rep"),
        check_vma=False,
    )
```

time: 282 us -> 212 us (0.75)
  Pallas kernels: 262 us -> 212 us
  local copies, waits for them, and re-layouts: 19.3 us -> 0 us
    pallas_call x1 -> x2, Pallas kernels: 262 us -> 212 us  [the longest x1 202 us: step(): pl.pallas_call(kernel, name='grad_sums', out_shape=pltpu.VMEM((n_mat, row...]
    unnamed x1 -> x0, local copies, waits for them, and re-layouts: 19.3 us -> none
where the time goes in v2:
time: 212 us
  Pallas kernels  212 us (100%)
    pallas_call x1, Pallas kernels, step(): pl.pallas_call(kernel, name='grad_sums', out_shape=pltpu.VMEM((n_mat, row...  202 us
    pallas_call x1, Pallas kernels, step(): pl.pallas_call(place, name='place', out_shape=jax.ShapeDtypeStruct(sums.s...  9.62 us

profile of v2, /device:TPU:0, one launch (start us, length us, event | category | flops | bytes accessed | tf_op | source)
XLA Modules:
  0.0 211.6 jit_solution(3722245963396036119)
XLA Ops:
  0.0 202.0 %grad_sums.1.src = bf16[4,1024,3328]{2,1,0:T(8,128)(2,1)S(1)} custom-call(bf16[1,4,4096,1024]{3,2,1,0:T(8,128)(2,1)} %a.1, bf16[1,4,4096,3328]{3,2,1,0:T(8,128)(2,1)} %g.1), custom_call_target="tpu_custom_call" | custom-call | flops 111669149696 | bytes 142606336 | tf_op jit(solution)/shard_map/grad_sums/pallas_call | solution.py:248
  202.0 9.6 %place.1 = bf16[4,1024,3328]{2,1,0:T(8,128)(2,1)} custom-call(bf16[4,1024,3328]{2,1,0:T(8,128)(2,1)S(1)} %grad_sums.1.src), custom_call_target="tpu_custom_call" | custom-call | tf_op jit(solution)/shard_map/place/pallas_call | solution.py:294
